TPU v7x, 32 devices: a whole 2x2x4 slice. The times are simulated.
32 devices in a mesh: band: 32 (over z, y, x, core).
Axes of the slice: x: 2, y: 2, z: 4, core: 2. Of those that a mesh axis runs over, the one named last changes fastest.
Arguments:
- jones_start: float32 [32, 32, 512], P('band'), may hold values from -1.5 to 1.5
- visible: bfloat16 [32, 8, 4096], P('band'), may hold values from -6 to 6
- coherent: bfloat16 [32, 32, 4096], P('band'), may hold values from -1 to 1
- stations: int32 [2, 4096], replicated, may hold values from 0 to 511, as said below
- weights: float32 [32, 512], P('band'), may hold values from 0.2 to 2
- multiplier_start: float32 [32, 32, 512], P('band'), may hold values from -2 to 2
Outputs:
- jones_final: float32 [32, 32, 512], P('band')
- multiplier_final: float32 [32, 32, 512], P('band')
- coefficients: float32 [96, 512], P(None, 'band')
Inputs may be any that keep to these rules, and one draw needn't show every extreme that they name: Rows 0 and 1 of each column name two different stations; the same baselines serve every subband.
All inputs are finite; a program needn't handle non-finite values.
Results may differ from a plain program's by a relative error of at most 0.0003.
Values sent between devices are 32-bit elements; how exact they have to be, the bound alone decides.
A program may use at most 64 MiB of HBM per device.

v0:
```python
import jax
import jax.numpy as jnp
from jax import lax
from jax.sharding import PartitionSpec as P

ITERS = 2
PENALTY = 1.0
STEP_SIZE = 0.05
PAIR_LIST = ((0, 0), (0, 1), (0, 2), (1, 1), (1, 2), (2, 2))


def matrix_product(first_real, first_imag, second_real, second_imag):

    def contract(lhs_part, rhs_part):
        return jnp.sum(lhs_part[:, :, :, None, :] * rhs_part[:, None, :, :, :], axis=2)

    real_part = contract(first_real, second_real) - contract(first_imag, second_imag)
    imag_part = contract(first_real, second_imag) + contract(first_imag, second_real)
    return (real_part, imag_part)


def band_loss(
    jones_band, visible_band, coherent_band, stations, target_band, multiplier_band, weight_band
):
    baseline_count = stations.shape[1]
    direction_count = jones_band.shape[0] // 8
    station_first = jnp.take(jones_band, stations[0], axis=1).reshape(
        direction_count, 2, 2, 2, baseline_count
    )
    station_second = jnp.take(jones_band, stations[1], axis=1).reshape(
        direction_count, 2, 2, 2, baseline_count
    )
    sky_model = coherent_band.astype(jnp.float32).reshape(direction_count, 2, 2, 2, baseline_count)
    inner_real, inner_imag = matrix_product(
        station_first[:, 0], station_first[:, 1], sky_model[:, 0], sky_model[:, 1]
    )
    herm_real = jnp.swapaxes(station_second[:, 0], 1, 2)
    herm_imag = -jnp.swapaxes(station_second[:, 1], 1, 2)
    model_real, model_imag = matrix_product(inner_real, inner_imag, herm_real, herm_imag)
    predicted = jnp.stack([jnp.sum(model_real, axis=0), jnp.sum(model_imag, axis=0)])
    misfit = visible_band.astype(jnp.float32).reshape(2, 2, 2, baseline_count) - predicted
    data_scale = jones_band.shape[1] / (2.0 * baseline_count)
    distance = jones_band - target_band
    return (
        data_scale * jnp.sum(misfit * misfit)
        + jnp.sum(multiplier_band * distance)
        + 0.5 * PENALTY * jnp.sum(weight_band[None, :] * distance * distance)
    )


def descend(
    jones_band, visible_band, coherent_band, stations, target_band, multiplier_band, weight_band
):
    slope_fn = jax.grad(band_loss)
    slope = slope_fn(
        jones_band, visible_band, coherent_band, stations, target_band, multiplier_band, weight_band
    )
    jones_band = jones_band - STEP_SIZE * slope
    return jones_band


def solve_normal(normal_matrix, right_side):
    gram_aa, gram_ab, gram_ac, gram_bb, gram_bc, gram_cc = [
        normal_matrix[position] for position in range(6)
    ]
    cofac_aa = gram_bb * gram_cc - gram_bc * gram_bc
    cofac_ab = gram_ac * gram_bc - gram_ab * gram_cc
    cofac_ac = gram_ab * gram_bc - gram_ac * gram_bb
    cofac_bb = gram_aa * gram_cc - gram_ac * gram_ac
    cofac_bc = gram_ab * gram_ac - gram_aa * gram_bc
    cofac_cc = gram_aa * gram_bb - gram_ab * gram_ab
    determinant = gram_aa * cofac_aa + gram_ab * cofac_ab + gram_ac * cofac_ac
    inverse_det = 1.0 / determinant
    first_term = right_side[0]
    second_term = right_side[1]
    third_term = right_side[2]
    coeff_a = (cofac_aa * first_term + cofac_ab * second_term + cofac_ac * third_term) * inverse_det
    coeff_b = (cofac_ab * first_term + cofac_bb * second_term + cofac_bc * third_term) * inverse_det
    coeff_c = (cofac_ac * first_term + cofac_bc * second_term + cofac_cc * third_term) * inverse_det
    return jnp.stack([coeff_a, coeff_b, coeff_c])


def local(jones_start, visible, coherent, stations, weights, multiplier_start):
    band_count = lax.axis_size("band")
    band_index = lax.axis_index("band")
    abscissa = -1.0 + 2.0 * band_index.astype(jnp.float32) / (band_count - 1)
    basis_local = (jnp.ones((), jnp.float32), abscissa, 1.5 * abscissa * abscissa - 0.5)
    weight_band = weights[0]
    visible_band = visible[0]
    coherent_band = coherent[0]
    station_share = weights.shape[1] // band_count
    products = jnp.stack(
        [basis_local[first_idx] * basis_local[second_idx] for first_idx, second_idx in PAIR_LIST]
    )
    normal_term = PENALTY * products[:, None] * weight_band[None, :]
    normal_solver = lax.psum(normal_term, "band")

    def iteration(turn_index, carried):
        jones_band, multiplier_band, owned_prior = carried
        combined = multiplier_band + PENALTY * weight_band[None, :] * jones_band
        weighted_terms = jnp.stack([basis_local[term_index] * combined for term_index in range(3)])
        full_sums = lax.psum(weighted_terms, "band")
        coefficients = solve_normal(normal_solver, full_sums)
        owned_coeff = lax.dynamic_slice_in_dim(
            coefficients, band_index * station_share, station_share, 2
        )
        target_band = (
            basis_local[0] * coefficients[0]
            + basis_local[1] * coefficients[1]
            + basis_local[2] * coefficients[2]
        )
        multiplier_band = multiplier_band + PENALTY * weight_band[None, :] * (
            jones_band - target_band
        )
        jones_band = descend(
            jones_band,
            visible_band,
            coherent_band,
            stations,
            target_band,
            multiplier_band,
            weight_band,
        )
        return (jones_band, multiplier_band, owned_coeff)

    owned_start = jnp.zeros((3, jones_start.shape[1], station_share), jnp.float32)
    jones_band, multiplier_band, owned_coeff = lax.fori_loop(
        0, ITERS, iteration, (jones_start[0], multiplier_start[0], owned_start)
    )
    coeff_rows = owned_coeff.reshape(
        owned_coeff.shape[0] * owned_coeff.shape[1], owned_coeff.shape[2]
    )
    return (jones_band[None], multiplier_band[None], coeff_rows)


def solution(mesh):
    return jax.shard_map(
        local,
        mesh=mesh,
        in_specs=(
            P("band", None, None),
            P("band", None, None),
            P("band", None, None),
            P(),
            P("band", None),
            P("band", None, None),
        ),
        out_specs=(P("band", None, None), P("band", None, None), P(None, "band")),
        check_vma=False,
    )
```

profile of v0, /device:TPU:8, one launch (start us, length us, event | category | flops | bytes accessed | tf_op | source)
XLA Modules:
  0.0 373.0 jit_solution(7236217893154198396)
XLA Ops:
  7.2 0.8 copy.133
  8.0 0.8 copy.134
  8.9 0.8 broadcast_multiply_fusion.1
  9.7 40.5 %psum.17 = f32[6,512]{1,0:T(8,128)S(1)} all-reduce(f32[6,512]{1,0:T(8,128)S(1)} %broadcast_multiply_fusion.1), channel_id=1, replica_groups=mesh['band'=32] {'band'}, use_global_device_ids=true, to_apply=%region_0.0 | all-reduce | flops 3072 | bytes 24576 | tf_op jit(solution)/shard_map/psum | solution.py:96
  50.1 0.6 multiply_add_fusion.2
  50.8 313.9 %while.17 = (s32[]{:T(128)}, f32[32,512]{1,0:T(8,128)S(1)}, f32[32,512]{1,0:T(8,128)S(1)}, f32[3,32,16]{2,1,0:T(8,128)}, f32[1,512]{1,0:T(1,128)}, /*index=5*/f3...) while((s32[]{:T(128)}, f32[32,512]{1,0:T(8,128)S(1)}, ...), condition=%wide.region_27.0_spmd, body=%wide.region_1.28_spmd.sunk | while | flops 6967298 | bytes 52347996 | solution.py:127
  50.8 0.7 multiply_bitcast_fusion.4
  51.5 0.7 pad_maximum_fusion.2
  52.3 0.9 fusion.32
  53.2 0.6 compare_select_fusion.3
  53.8 14.1 %gather_fusion.1 = f32[4096,32]{1,0:T(8,128)} fusion(f32[32,512]{0,1:T(8,128)S(1)} %copy.101, s32[4096]{0:T(1024)S(1)} %get-tuple-element.581), kind=kCustom, calls=%fused_computation.1.clone.clone.1 | custom fusion | bytes 1064960 | tf_op jit(solution)/shard_map/while/body/eval_jaxpr/jvp(jit(_take))/gather | solution.py:27
  67.9 3.6 select_bitcast_fusion.5
  71.5 0.6 copy.105
  72.5 0.9 copy.106
  73.4 0.9 copy.108
  74.3 0.3 reshape.303
  75.0 14.1 %gather_fusion = f32[4096,32]{1,0:T(8,128)} fusion(f32[32,512]{0,1:T(8,128)S(1)} %copy.101, s32[4096]{0:T(1024)S(1)} %get-tuple-element.578), kind=kCustom, calls=%fused_computation.clone.clone.1 | custom fusion | bytes 1064960 | tf_op jit(solution)/shard_map/while/body/eval_jaxpr/jvp(jit(_take))/gather | solution.py:30
  89.1 3.6 select_bitcast_fusion.4
  92.7 0.6 copy.103
  94.4 0.6 multiply_reduce_fusion.24
  95.2 0.6 multiply_reduce_fusion.25
  95.8 0.5 add_reduce_fusion.2
  96.4 1.3 multiply_reduce_fusion.26
  97.9 0.6 multiply_reduce_fusion.27
  99.3 0.4 copy.113
  99.7 0.4 reshape.305
  100.1 2.0 copy.114
  102.0 0.4 copy.111
  102.5 0.4 reshape.304
  102.9 0.6 copy.112
  103.5 22.7 %scatter_custom_fusion.8 = f32[32,512]{0,1:T(8,128)S(1)} fusion(s32[4096]{0:T(1024)} %get-tuple-element.603, f32[4096,32]{1,0:T(8,128)} %copy.114, f32[]{:T(128)} %constant.70.clone.25..sunk), kind=kCustom, calls=%fused_computation.50.clone.1 | custom fusion | flops 131072 | bytes 66048 | tf_op jit(solution)/shard_map/while/body/eval_jaxpr/transpose(jvp(jit(_take)))/scatter-add | solution.py:27
  126.2 57.3 %all-reduce.6.cloned.1.call-done = f32[3,32,512]{2,1,0:T(8,128)} async-done(((f32[3,32,512]{2,1,0:T(8,128)}), f32[3,32,512]{2,1,0:T(8,128)}) %all-reduce.6.cloned.1.call-update) | async-done | bytes 196624 | tf_op jit(solution)/shard_map/while/body/eval_jaxpr/psum | solution.py:102
  183.5 1.0 add_add_fusion.2
  184.7 22.5 %scatter_fusion = f32[32,512]{0,1:T(8,128)S(1)} fusion(f32[32,512]{0,1:T(8,128)S(1)} %copy.102, s32[4096]{0:T(1024)S(1)} %get-tuple-element.577, f32[4096,32]{1,0:T(8,128)S(1)} %copy.112), kind=kCustom, calls=%fused_computation.2.clone.1 | custom fusion | flops 131072 | bytes 1589248 | tf_op jit(solution)/shard_map/while/body/eval_jaxpr/transpose(jvp(jit(_take)))/scatter-add | solution.py:30
  207.4 0.7 fusion.36
  208.1 0.7 multiply_bitcast_fusion.4
  208.8 0.7 pad_maximum_fusion.2
  209.6 0.9 fusion.32
  210.5 0.6 compare_select_fusion.3
  211.2 14.1 %gather_fusion.1 = f32[4096,32]{1,0:T(8,128)} fusion(f32[32,512]{0,1:T(8,128)S(1)} %copy.101, s32[4096]{0:T(1024)S(1)} %get-tuple-element.581), kind=kCustom, calls=%fused_computation.1.clone.clone.1 | custom fusion | bytes 1064960 | tf_op jit(solution)/shard_map/while/body/eval_jaxpr/jvp(jit(_take))/gather | solution.py:27
  225.3 3.6 select_bitcast_fusion.5
  228.9 0.6 copy.105
  229.8 0.9 copy.106
  230.7 0.9 copy.108
  232.3 14.1 %gather_fusion = f32[4096,32]{1,0:T(8,128)} fusion(f32[32,512]{0,1:T(8,128)S(1)} %copy.101, s32[4096]{0:T(1024)S(1)} %get-tuple-element.578), kind=kCustom, calls=%fused_computation.clone.clone.1 | custom fusion | bytes 1064960 | tf_op jit(solution)/shard_map/while/body/eval_jaxpr/jvp(jit(_take))/gather | solution.py:30
  246.4 3.6 select_bitcast_fusion.4
  250.0 0.6 copy.103
  251.7 0.6 multiply_reduce_fusion.24
  252.5 0.6 multiply_reduce_fusion.25
  253.1 0.5 add_reduce_fusion.2
  253.8 1.3 multiply_reduce_fusion.26
  255.2 0.6 multiply_reduce_fusion.27
  256.6 0.4 copy.113
  257.0 0.4 reshape.305
  257.4 2.0 copy.114
  259.4 0.4 copy.111
  259.8 0.4 reshape.304
  260.2 0.6 copy.112
  260.8 22.7 %scatter_custom_fusion.8 = f32[32,512]{0,1:T(8,128)S(1)} fusion(s32[4096]{0:T(1024)} %get-tuple-element.603, f32[4096,32]{1,0:T(8,128)} %copy.114, f32[]{:T(128)} %constant.70.clone.25..sunk), kind=kCustom, calls=%fused_computation.50.clone.1 | custom fusion | flops 131072 | bytes 66048 | tf_op jit(solution)/shard_map/while/body/eval_jaxpr/transpose(jvp(jit(_take)))/scatter-add | solution.py:27
  283.5 56.6 %all-reduce.6.cloned.1.call-done = f32[3,32,512]{2,1,0:T(8,128)} async-done(((f32[3,32,512]{2,1,0:T(8,128)}), f32[3,32,512]{2,1,0:T(8,128)}) %all-reduce.6.cloned.1.call-update) | async-done | bytes 196624 | tf_op jit(solution)/shard_map/while/body/eval_jaxpr/psum | solution.py:102
  340.1 1.0 add_add_fusion.2
  341.3 22.5 %scatter_fusion = f32[32,512]{0,1:T(8,128)S(1)} fusion(f32[32,512]{0,1:T(8,128)S(1)} %copy.102, s32[4096]{0:T(1024)S(1)} %get-tuple-element.577, f32[4096,32]{1,0:T(8,128)S(1)} %copy.112), kind=kCustom, calls=%fused_computation.2.clone.1 | custom fusion | flops 131072 | bytes 1589248 | tf_op jit(solution)/shard_map/while/body/eval_jaxpr/transpose(jvp(jit(_take)))/scatter-add | solution.py:30
  364.0 0.7 fusion.36
  364.7 1.5 copy.85
  (131 shorter events, 7.3 us)
Async XLA Ops:
  50.8 132.8 %all-reduce.6.cloned.1.call-start = ((), (), s32[]{:S(2)}) async-start(), calls=%async_computation | async-start | bytes 393216 | tf_op jit(solution)/shard_map/while/body/eval_jaxpr/psum | solution.py:102
  72.1 2.1 copy-start.5
  93.3 0.8 copy-start.6
  93.3 1.0 copy-start
  93.3 1.1 copy-start.1
  95.1 1.3 copy-start.7
  98.6 0.7 copy-start.14
  102.4 81.1 %copy-start.8 = (f32[1,512]{1,0:T(1,128)S(1)}, f32[1,512]{1,0:T(1,128)}, u32[]{:S(2)}) copy-start(f32[1,512]{1,0:T(1,128)} %get-tuple-element.667) | copy-start | bytes 6148 | tf_op jit(solution)/shard_map/while
  102.4 81.1 %copy-start.9 = (f32[1,512]{1,0:T(1,128)S(1)}, f32[1,512]{1,0:T(1,128)}, u32[]{:S(2)}) copy-start(f32[1,512]{1,0:T(1,128)} %get-tuple-element.666) | copy-start | bytes 6148 | tf_op jit(solution)/shard_map/while
  102.4 81.1 %copy-start.10 = (f32[1,512]{1,0:T(1,128)S(1)}, f32[1,512]{1,0:T(1,128)}, u32[]{:S(2)}) copy-start(f32[1,512]{1,0:T(1,128)} %get-tuple-element.663) | copy-start | bytes 6148 | tf_op jit(solution)/shard_map/while
  102.5 81.1 %copy-start.11 = (f32[1,512]{1,0:T(1,128)S(1)}, f32[1,512]{1,0:T(1,128)}, u32[]{:S(2)}) copy-start(f32[1,512]{1,0:T(1,128)} %get-tuple-element.671) | copy-start | bytes 6148 | tf_op jit(solution)/shard_map/while
  102.5 81.1 %copy-start.12 = (f32[1,512]{1,0:T(1,128)S(1)}, f32[1,512]{1,0:T(1,128)}, u32[]{:S(2)}) copy-start(f32[1,512]{1,0:T(1,128)} %get-tuple-element.670) | copy-start | bytes 6148 | tf_op jit(solution)/shard_map/while
  102.5 81.1 %copy-start.13 = (f32[1,512]{1,0:T(1,128)S(1)}, f32[1,512]{1,0:T(1,128)}, u32[]{:S(2)}) copy-start(f32[1,512]{1,0:T(1,128)} %get-tuple-element.669) | copy-start | bytes 6148 | tf_op jit(solution)/shard_map/while
  184.7 22.7 %copy-start.2 = (f32[3,32,512]{2,1,0:T(8,128)S(1)}, f32[3,32,512]{2,1,0:T(8,128)}, u32[]{:S(2)}) copy-start(f32[3,32,512]{2,1,0:T(8,128)} %all-reduce.6.cloned.1.call-done) | copy-start | bytes 589828 | tf_op jit(solution)/shard_map/while
  208.1 132.0 %all-reduce.6.cloned.1.call-start = ((), (), s32[]{:S(2)}) async-start(), calls=%async_computation | async-start | bytes 393216 | tf_op jit(solution)/shard_map/while/body/eval_jaxpr/psum | solution.py:102
  229.4 2.1 copy-start.5
  250.6 0.8 copy-start.6
  250.6 1.0 copy-start
  250.6 1.1 copy-start.1
  252.5 1.3 copy-start.7
  255.9 0.7 copy-start.14
  259.8 80.3 %copy-start.8 = (f32[1,512]{1,0:T(1,128)S(1)}, f32[1,512]{1,0:T(1,128)}, u32[]{:S(2)}) copy-start(f32[1,512]{1,0:T(1,128)} %get-tuple-element.667) | copy-start | bytes 6148 | tf_op jit(solution)/shard_map/while
  259.8 80.3 %copy-start.9 = (f32[1,512]{1,0:T(1,128)S(1)}, f32[1,512]{1,0:T(1,128)}, u32[]{:S(2)}) copy-start(f32[1,512]{1,0:T(1,128)} %get-tuple-element.666) | copy-start | bytes 6148 | tf_op jit(solution)/shard_map/while
  259.8 80.3 %copy-start.10 = (f32[1,512]{1,0:T(1,128)S(1)}, f32[1,512]{1,0:T(1,128)}, u32[]{:S(2)}) copy-start(f32[1,512]{1,0:T(1,128)} %get-tuple-element.663) | copy-start | bytes 6148 | tf_op jit(solution)/shard_map/while
  259.8 80.3 %copy-start.11 = (f32[1,512]{1,0:T(1,128)S(1)}, f32[1,512]{1,0:T(1,128)}, u32[]{:S(2)}) copy-start(f32[1,512]{1,0:T(1,128)} %get-tuple-element.671) | copy-start | bytes 6148 | tf_op jit(solution)/shard_map/while
  259.8 80.3 %copy-start.12 = (f32[1,512]{1,0:T(1,128)S(1)}, f32[1,512]{1,0:T(1,128)}, u32[]{:S(2)}) copy-start(f32[1,512]{1,0:T(1,128)} %get-tuple-element.670) | copy-start | bytes 6148 | tf_op jit(solution)/shard_map/while
  259.8 80.3 %copy-start.13 = (f32[1,512]{1,0:T(1,128)S(1)}, f32[1,512]{1,0:T(1,128)}, u32[]{:S(2)}) copy-start(f32[1,512]{1,0:T(1,128)} %get-tuple-element.669) | copy-start | bytes 6148 | tf_op jit(solution)/shard_map/while
  341.3 22.7 %copy-start.2 = (f32[3,32,512]{2,1,0:T(8,128)S(1)}, f32[3,32,512]{2,1,0:T(8,128)}, u32[]{:S(2)}) copy-start(f32[3,32,512]{2,1,0:T(8,128)} %all-reduce.6.cloned.1.call-done) | copy-start | bytes 589828 | tf_op jit(solution)/shard_map/while
  364.7 1.5 copy-start.3
  364.7 1.5 copy-start.4
Sparse Core Ops, SparseCore 0:
  57.1 126.3 all-reduce.5
  214.4 125.6 all-reduce.5
where the time goes:
time: 374 us; the launch traced here: 373 us
  other arithmetic  123 us (33%)
  waiting for transfers between devices  114 us (30%)
  local copies, waits for them, and re-layouts  80.8 us (22%)
  blocking collectives  40.5 us (11%)
  between operations  14 us (4%)
    psum x2, waiting for transfers between devices, iteration(): full_sums = lax.psum(weighted_terms, 'band')  114 us
    scatter-add x2, other arithmetic, band_loss(): jnp.take(jones_band, stations[0], axis=1)  45.4 us
    scatter-add x2, other arithmetic, band_loss(): jnp.take(jones_band, stations[1], axis=1)  45 us
    psum x1, blocking collectives, local(): normal_solver = lax.psum(normal_term, 'band')  40.5 us
    gather x2, local copies, waits for them, and re-layouts, band_loss(): jnp.take(jones_band, stations[0], axis=1)  28.2 us
    gather x2, local copies, waits for them, and re-layouts, band_loss(): jnp.take(jones_band, stations[1], axis=1)  28.2 us
    select_n x4, other arithmetic, band_loss(): jnp.take(jones_band, stations[0], axis=1)  8.44 us
  transfers between devices with their start and end apart: 2, of which 2 were waited for; matrix products, arithmetic and copies ran while one was open for 39% of the time, Pallas kernels for 0%

commit v1 on v0

--- a/solution.py
+++ b/solution.py
@@ -99,7 +99,11 @@
         jones_band, multiplier_band, owned_prior = carried
         combined = multiplier_band + PENALTY * weight_band[None, :] * jones_band
         weighted_terms = jnp.stack([basis_local[term_index] * combined for term_index in range(3)])
-        full_sums = lax.psum(weighted_terms, "band")
+        full_sums = weighted_terms
+        for hop in (1, 2, 4, 8, 16):
+            full_sums = full_sums + lax.ppermute(
+                full_sums, "band", [(dev, dev ^ hop) for dev in range(32)]
+            )
         coefficients = solve_normal(normal_solver, full_sums)
         owned_coeff = lax.dynamic_slice_in_dim(
             coefficients, band_index * station_share, station_share, 2

time: 374 us -> 310 us (0.83); the launches traced: 373 us -> 305 us
  waiting for transfers between devices: 114 us -> 36.4 us
  between operations: 14 us -> 0.63 us
  starting transfers between devices: 0.01 us -> 12.8 us
  other arithmetic: 123 us -> 128 us
  local copies, waits for them, and re-layouts: 80.8 us -> 85.2 us
    psum x2 -> x0, waiting for transfers between devices: 114 us -> none  [iteration(): full_sums = lax.psum(weighted_terms, 'band')]
    ppermute x0 -> x10, waiting for transfers between devices: none -> 36.4 us  [iteration(): lax.ppermute(full_sums, 'band', [(dev, dev ^ hop) for dev in range(32)])]
    ppermute x0 -> x10, starting transfers between devices: none -> 12.8 us  [iteration(): lax.ppermute(full_sums, 'band', [(dev, dev ^ hop) for dev in range(32)])]
    add x0 -> x10, other arithmetic: none -> 4.02 us  [iteration(): full_sums + lax.ppermute(full_sums, 'band', [(dev, dev ^ hop) for dev in...]
  transfers between devices with their start and end apart: 2 -> 10, of which waited for: 2 -> 6; matrix products, arithmetic and copies ran while one was open for 39% -> 48% of each run, Pallas kernels for 0% -> 0%
where the time goes in v1:
time: 310 us; the launch traced here: 305 us
  other arithmetic  128 us (41%)
  local copies, waits for them, and re-layouts  85.2 us (27%)
  blocking collectives  40.5 us (13%)
  waiting for transfers between devices  36.4 us (12%)
  starting transfers between devices  12.8 us (4%)
    scatter-add x2, other arithmetic, band_loss(): jnp.take(jones_band, stations[0], axis=1)  45.4 us
    scatter-add x2, other arithmetic, band_loss(): jnp.take(jones_band, stations[1], axis=1)  45 us
    psum x1, blocking collectives, local(): normal_solver = lax.psum(normal_term, 'band')  40.5 us
    ppermute x10, waiting for transfers between devices, iteration(): lax.ppermute(full_sums, 'band', [(dev, dev ^ hop) for dev in range(32)])  36.4 us
    gather x2, local copies, waits for them, and re-layouts, band_loss(): jnp.take(jones_band, stations[0], axis=1)  28.2 us
    gather x2, local copies, waits for them, and re-layouts, band_loss(): jnp.take(jones_band, stations[1], axis=1)  28.2 us
    ppermute x10, starting transfers between devices, iteration(): lax.ppermute(full_sums, 'band', [(dev, dev ^ hop) for dev in range(32)])  12.8 us
    select_n x4, other arithmetic, band_loss(): jnp.take(jones_band, stations[0], axis=1)  8.41 us
  transfers between devices with their start and end apart: 10, of which 6 were waited for; matrix products, arithmetic and copies ran while one was open for 48% of the time, Pallas kernels for 0%

profile of v1, /device:TPU:8, one launch (start us, length us, event | category | flops | bytes accessed | tf_op | source)
XLA Modules:
  0.0 305.1 jit_solution(10061512193636918298)
XLA Ops:
  0.6 1.5 copy.151
  2.1 1.5 copy.152
  3.7 0.8 broadcast_multiply_fusion.1
  4.4 40.5 %psum.7 = f32[6,512]{1,0:T(8,128)S(1)} all-reduce(f32[6,512]{1,0:T(8,128)S(1)} %broadcast_multiply_fusion.1), channel_id=1, replica_groups=mesh['band'=32] {'band'}, use_global_device_ids=true, to_apply=%region_0.0 | all-reduce | flops 3072 | bytes 24576 | tf_op jit(solution)/shard_map/psum | solution.py:96
  44.9 0.6 multiply_add_fusion.2
  45.5 258.1 %while.17 = (s32[]{:T(128)}, f32[32,512]{1,0:T(8,128)}, f32[32,512]{1,0:T(8,128)}, f32[3,32,16]{2,1,0:T(8,128)}, f32[1,512]{1,0:T(1,128)}, /*index=5*/f32[1,512]...) while((s32[]{:T(128)}, f32[32,512]{1,0:T(8,128)}, ...), condition=%wide.region_26.0_spmd, body=%wide.region_1.27_spmd.sunk | while | flops 7409666 | bytes 57984280 | solution.py:131
  45.5 0.9 multiply_bitcast_fusion.4
  46.4 0.7 pad_maximum_fusion.2
  47.1 1.0 copy.120
  48.1 0.9 fusion.38
  49.6 14.1 %gather_fusion.1 = f32[4096,32]{1,0:T(8,128)} fusion(f32[32,512]{0,1:T(8,128)S(1)} %copy.120, s32[4096]{0:T(1024)S(1)} %get-tuple-element.581), kind=kCustom, calls=%fused_computation.1.clone.clone.1 | custom fusion | bytes 1064960 | tf_op jit(solution)/shard_map/while/body/eval_jaxpr/jvp(jit(_take))/gather | solution.py:27
  63.7 3.6 %select_bitcast_fusion.5 = f32[32,4096]{0,1:T(8,128)S(1)} fusion(f32[4096,32]{1,0:T(8,128)} %gather_fusion.1, pred[4096]{0:T(1024)(128)(4,1)S(1)} %compare_and_fusion.5), kind=kLoop, calls=%fused_computation.4.clone.1 | loop fusion | flops 131072 | bytes 1052672 | tf_op jit(solution)/shard_map/while/body/eval_jaxpr/jvp(jit(_take))/select_n | solution.py:27
  68.2 0.9 copy.125
  69.1 0.9 copy.127
  70.8 14.1 %gather_fusion = f32[4096,32]{1,0:T(8,128)} fusion(f32[32,512]{0,1:T(8,128)S(1)} %copy.120, s32[4096]{0:T(1024)S(1)} %get-tuple-element.578), kind=kCustom, calls=%fused_computation.clone.clone.1 | custom fusion | bytes 1064960 | tf_op jit(solution)/shard_map/while/body/eval_jaxpr/jvp(jit(_take))/gather | solution.py:30
  84.9 3.6 %select_bitcast_fusion.4 = f32[32,4096]{0,1:T(8,128)S(1)} fusion(f32[4096,32]{1,0:T(8,128)} %gather_fusion, pred[4096]{0:T(1024)(128)(4,1)S(1)} %compare_and_fusion.4), kind=kLoop, calls=%fused_computation.5.clone.1 | loop fusion | flops 131072 | bytes 1052672 | tf_op jit(solution)/shard_map/while/body/eval_jaxpr/jvp(jit(_take))/select_n | solution.py:30
  90.1 0.6 multiply_reduce_fusion.24
  90.9 0.6 multiply_reduce_fusion.25
  92.2 1.3 multiply_reduce_fusion.26
  93.6 0.6 multiply_reduce_fusion.27
  95.1 1.0 fusion.36
  96.0 2.3 collective-permute-start.1
  98.4 5.5 %collective-permute-done.1 = f32[3,32,512]{2,1,0:T(8,128)S(1)} collective-permute-done((f32[3,32,512]{2,1,0:T(8,128)S(1)}, f32[3,32,512]{2,1,0:T(8,128)S(1)}, u32[]{:S(2)}, u32[]{:S(2)}) %collective-permute-start.1) | collective-permute-done | bytes 196640 | tf_op jit(solution)/shard_map/while/body/eval_jaxpr/ppermute | solution.py:104
  103.9 1.0 fusion.37
  104.9 1.8 collective-permute-start.2
  107.6 2.0 copy.133
  111.0 22.7 %scatter_custom_fusion.8 = f32[32,512]{0,1:T(8,128)S(1)} fusion(s32[4096]{0:T(1024)} %get-tuple-element.603, f32[4096,32]{1,0:T(8,128)} %copy.133, f32[]{:T(128)} %constant.70.clone.25..sunk), kind=kCustom, calls=%fused_computation.50.clone.1 | custom fusion | flops 131072 | bytes 66048 | tf_op jit(solution)/shard_map/while/body/eval_jaxpr/transpose(jvp(jit(_take)))/scatter-add | solution.py:27
  134.4 5.6 %collective-permute-done.3 = f32[3,32,512]{2,1,0:T(8,128)S(1)} collective-permute-done((f32[3,32,512]{2,1,0:T(8,128)S(1)}, f32[3,32,512]{2,1,0:T(8,128)S(1)}, u32[]{:S(2)}, u32[]{:S(2)}) %collective-permute-start.3) | collective-permute-done | bytes 196640 | tf_op jit(solution)/shard_map/while/body/eval_jaxpr/ppermute | solution.py:104
  140.0 1.3 collective-permute-start.4
  141.4 7.0 %collective-permute-done.4 = f32[3,32,512]{2,1,0:T(8,128)S(1)} collective-permute-done((f32[3,32,512]{2,1,0:T(8,128)S(1)}, f32[3,32,512]{2,1,0:T(8,128)S(1)}, u32[]{:S(2)}, u32[]{:S(2)}) %collective-permute-start.4) | collective-permute-done | bytes 196640 | tf_op jit(solution)/shard_map/while/body/eval_jaxpr/ppermute | solution.py:104
  148.6 1.6 add_add_fusion.2
  150.3 22.5 %scatter_fusion = f32[32,512]{0,1:T(8,128)S(1)} fusion(f32[32,512]{0,1:T(8,128)S(1)} %copy.121, s32[4096]{0:T(1024)S(1)} %get-tuple-element.577, f32[4096,32]{1,0:T(8,128)S(1)} %copy.131), kind=kCustom, calls=%fused_computation.2.clone.1 | custom fusion | flops 131072 | bytes 1589248 | tf_op jit(solution)/shard_map/while/body/eval_jaxpr/transpose(jvp(jit(_take)))/scatter-add | solution.py:30
  172.8 0.7 copy.134
  173.6 0.7 fusion.42
  174.3 0.9 multiply_bitcast_fusion.4
  175.2 0.7 pad_maximum_fusion.2
  175.9 1.0 copy.120
  176.8 0.9 fusion.38
  178.4 14.1 %gather_fusion.1 = f32[4096,32]{1,0:T(8,128)} fusion(f32[32,512]{0,1:T(8,128)S(1)} %copy.120, s32[4096]{0:T(1024)S(1)} %get-tuple-element.581), kind=kCustom, calls=%fused_computation.1.clone.clone.1 | custom fusion | bytes 1064960 | tf_op jit(solution)/shard_map/while/body/eval_jaxpr/jvp(jit(_take))/gather | solution.py:27
  192.4 3.6 %select_bitcast_fusion.5 = f32[32,4096]{0,1:T(8,128)S(1)} fusion(f32[4096,32]{1,0:T(8,128)} %gather_fusion.1, pred[4096]{0:T(1024)(128)(4,1)S(1)} %compare_and_fusion.5), kind=kLoop, calls=%fused_computation.4.clone.1 | loop fusion | flops 131072 | bytes 1052672 | tf_op jit(solution)/shard_map/while/body/eval_jaxpr/jvp(jit(_take))/select_n | solution.py:27
  197.0 0.9 copy.125
  197.9 0.9 copy.127
  199.5 14.1 %gather_fusion = f32[4096,32]{1,0:T(8,128)} fusion(f32[32,512]{0,1:T(8,128)S(1)} %copy.120, s32[4096]{0:T(1024)S(1)} %get-tuple-element.578), kind=kCustom, calls=%fused_computation.clone.clone.1 | custom fusion | bytes 1064960 | tf_op jit(solution)/shard_map/while/body/eval_jaxpr/jvp(jit(_take))/gather | solution.py:30
  213.6 3.6 %select_bitcast_fusion.4 = f32[32,4096]{0,1:T(8,128)S(1)} fusion(f32[4096,32]{1,0:T(8,128)} %gather_fusion, pred[4096]{0:T(1024)(128)(4,1)S(1)} %compare_and_fusion.4), kind=kLoop, calls=%fused_computation.5.clone.1 | loop fusion | flops 131072 | bytes 1052672 | tf_op jit(solution)/shard_map/while/body/eval_jaxpr/jvp(jit(_take))/select_n | solution.py:30
  218.9 0.6 multiply_reduce_fusion.24
  219.7 0.6 multiply_reduce_fusion.25
  220.9 1.3 multiply_reduce_fusion.26
  222.4 0.6 multiply_reduce_fusion.27
  223.8 1.0 fusion.36
  224.8 0.6 collective-permute-start.1
  225.4 6.7 %collective-permute-done.1 = f32[3,32,512]{2,1,0:T(8,128)S(1)} collective-permute-done((f32[3,32,512]{2,1,0:T(8,128)S(1)}, f32[3,32,512]{2,1,0:T(8,128)S(1)}, u32[]{:S(2)}, u32[]{:S(2)}) %collective-permute-start.1) | collective-permute-done | bytes 196640 | tf_op jit(solution)/shard_map/while/body/eval_jaxpr/ppermute | solution.py:104
  232.2 1.0 fusion.37
  233.1 0.9 collective-permute-start.2
  234.8 2.0 copy.133
  238.3 22.7 %scatter_custom_fusion.8 = f32[32,512]{0,1:T(8,128)S(1)} fusion(s32[4096]{0:T(1024)} %get-tuple-element.603, f32[4096,32]{1,0:T(8,128)} %copy.133, f32[]{:T(128)} %constant.70.clone.25..sunk), kind=kCustom, calls=%fused_computation.50.clone.1 | custom fusion | flops 131072 | bytes 66048 | tf_op jit(solution)/shard_map/while/body/eval_jaxpr/transpose(jvp(jit(_take)))/scatter-add | solution.py:27
  261.0 2.7 collective-permute-start.3
  263.8 4.4 %collective-permute-done.3 = f32[3,32,512]{2,1,0:T(8,128)S(1)} collective-permute-done((f32[3,32,512]{2,1,0:T(8,128)S(1)}, f32[3,32,512]{2,1,0:T(8,128)S(1)}, u32[]{:S(2)}, u32[]{:S(2)}) %collective-permute-start.3) | collective-permute-done | bytes 196640 | tf_op jit(solution)/shard_map/while/body/eval_jaxpr/ppermute | solution.py:104
  268.2 2.5 collective-permute-start.4
  270.8 7.0 %collective-permute-done.4 = f32[3,32,512]{2,1,0:T(8,128)S(1)} collective-permute-done((f32[3,32,512]{2,1,0:T(8,128)S(1)}, f32[3,32,512]{2,1,0:T(8,128)S(1)}, u32[]{:S(2)}, u32[]{:S(2)}) %collective-permute-start.4) | collective-permute-done | bytes 196640 | tf_op jit(solution)/shard_map/while/body/eval_jaxpr/ppermute | solution.py:104
  278.0 1.6 add_add_fusion.2
  279.7 22.5 %scatter_fusion = f32[32,512]{0,1:T(8,128)S(1)} fusion(f32[32,512]{0,1:T(8,128)S(1)} %copy.121, s32[4096]{0:T(1024)S(1)} %get-tuple-element.577, f32[4096,32]{1,0:T(8,128)S(1)} %copy.131), kind=kCustom, calls=%fused_computation.2.clone.1 | custom fusion | flops 131072 | bytes 1589248 | tf_op jit(solution)/shard_map/while/body/eval_jaxpr/transpose(jvp(jit(_take)))/scatter-add | solution.py:30
  302.2 0.7 copy.134
  302.9 0.7 fusion.42
  303.6 1.5 copy.104
  (155 shorter events, 16.8 us)
Async XLA Ops:
  46.4 0.7 copy-start
  47.1 47.5 %collective-permute-start = (f32[3,32,512]{2,1,0:T(8,128)}, f32[3,32,512]{2,1,0:T(8,128)}, u32[]{:S(2)}, u32[]{:S(2)}) collective-permute-start(f32[3,32,512]{2,1,0:T(8,128)} %pad_maximum_fusion.2), channel_id=1, source_target_pairs={{0,1},{1,0},{2,3},{3,2},{4,5},{5,4},{6,7},{7,6},{8,9},{9,8},{10,11... | collective-permute-start | bytes 589832 | tf_op jit(solution)/shard_map/while/body/eval_jaxpr/ppermute | solution.py:104
  67.9 2.1 copy-start.4
  89.0 0.8 copy-start.5
  89.0 1.0 copy-start.2
  89.1 1.1 copy-start.3
  94.2 0.8 copy-start.1
  96.0 7.9 %collective-permute-start.1 = (f32[3,32,512]{2,1,0:T(8,128)S(1)}, f32[3,32,512]{2,1,0:T(8,128)S(1)}, u32[]{:S(2)}, u32[]{:S(2)}) collective-permute-start(f32[3,32,512]{2,1,0:T(8,128)S(1)} %fusion.36), channel_id=1, source_target_pairs={{0,2},{1,3},{2,0},{3,1},{4,6},{5,7},{6,4},{7,5},{8,10},{9,11},{10,... | collective-permute-start | bytes 589832 | tf_op jit(solution)/shard_map/while/body/eval_jaxpr/ppermute | solution.py:104
  104.9 28.8 %collective-permute-start.2 = (f32[3,32,512]{2,1,0:T(8,128)S(1)}, f32[3,32,512]{2,1,0:T(8,128)S(1)}, u32[]{:S(2)}, u32[]{:S(2)}) collective-permute-start(f32[3,32,512]{2,1,0:T(8,128)S(1)} %fusion.37), channel_id=1, source_target_pairs={{0,4},{1,5},{2,6},{3,7},{4,0},{5,1},{6,2},{7,3},{8,12},{9,13},{10,... | collective-permute-start | bytes 589832 | tf_op jit(solution)/shard_map/while/body/eval_jaxpr/ppermute | solution.py:104
  109.9 24.4 %copy-start.6 = (f32[1,512]{1,0:T(1,128)S(1)}, f32[1,512]{1,0:T(1,128)}, u32[]{:S(2)}) copy-start(f32[1,512]{1,0:T(1,128)} %get-tuple-element.662) | copy-start | bytes 6148 | tf_op jit(solution)/shard_map/while
  110.3 31.1 %copy-start.13 = (f32[1,512]{1,0:T(1,128)S(1)}, f32[1,512]{1,0:T(1,128)}, u32[]{:S(2)}) copy-start(f32[1,512]{1,0:T(1,128)} %get-tuple-element.668) | copy-start | bytes 6148 | tf_op jit(solution)/shard_map/while
  110.3 38.1 %copy-start.7 = (f32[1,512]{1,0:T(1,128)S(1)}, f32[1,512]{1,0:T(1,128)}, u32[]{:S(2)}) copy-start(f32[1,512]{1,0:T(1,128)} %get-tuple-element.667) | copy-start | bytes 6148 | tf_op jit(solution)/shard_map/while
  110.3 38.1 %copy-start.8 = (f32[1,512]{1,0:T(1,128)S(1)}, f32[1,512]{1,0:T(1,128)}, u32[]{:S(2)}) copy-start(f32[1,512]{1,0:T(1,128)} %get-tuple-element.666) | copy-start | bytes 6148 | tf_op jit(solution)/shard_map/while
  110.3 38.1 %copy-start.9 = (f32[1,512]{1,0:T(1,128)S(1)}, f32[1,512]{1,0:T(1,128)}, u32[]{:S(2)}) copy-start(f32[1,512]{1,0:T(1,128)} %get-tuple-element.663) | copy-start | bytes 6148 | tf_op jit(solution)/shard_map/while
  110.4 38.1 %copy-start.10 = (f32[1,512]{1,0:T(1,128)S(1)}, f32[1,512]{1,0:T(1,128)}, u32[]{:S(2)}) copy-start(f32[1,512]{1,0:T(1,128)} %get-tuple-element.671) | copy-start | bytes 6148 | tf_op jit(solution)/shard_map/while
  110.4 38.1 %copy-start.11 = (f32[1,512]{1,0:T(1,128)S(1)}, f32[1,512]{1,0:T(1,128)}, u32[]{:S(2)}) copy-start(f32[1,512]{1,0:T(1,128)} %get-tuple-element.670) | copy-start | bytes 6148 | tf_op jit(solution)/shard_map/while
  110.4 38.1 %copy-start.12 = (f32[1,512]{1,0:T(1,128)S(1)}, f32[1,512]{1,0:T(1,128)}, u32[]{:S(2)}) copy-start(f32[1,512]{1,0:T(1,128)} %get-tuple-element.669) | copy-start | bytes 6148 | tf_op jit(solution)/shard_map/while
  133.8 6.2 %collective-permute-start.3 = (f32[3,32,512]{2,1,0:T(8,128)S(1)}, f32[3,32,512]{2,1,0:T(8,128)S(1)}, u32[]{:S(2)}, u32[]{:S(2)}) collective-permute-start(f32[3,32,512]{2,1,0:T(8,128)S(1)} %add.313), channel_id=1, source_target_pairs={{0,8},{1,9},{2,10},{3,11},{4,12},{5,13},{6,14},{7,15},{8,0},{9,1},... | collective-permute-start | bytes 589832 | tf_op jit(solution)/shard_map/while/body/eval_jaxpr/ppermute | solution.py:104
  140.0 8.4 %collective-permute-start.4 = (f32[3,32,512]{2,1,0:T(8,128)S(1)}, f32[3,32,512]{2,1,0:T(8,128)S(1)}, u32[]{:S(2)}, u32[]{:S(2)}) collective-permute-start(f32[3,32,512]{2,1,0:T(8,128)S(1)} %add.314), channel_id=1, source_target_pairs={{0,16},{1,17},{2,18},{3,19},{4,20},{5,21},{6,22},{7,23},{8,24},{9,... | collective-permute-start | bytes 589832 | tf_op jit(solution)/shard_map/while/body/eval_jaxpr/ppermute | solution.py:104
  175.2 0.7 copy-start
  175.9 47.5 %collective-permute-start = (f32[3,32,512]{2,1,0:T(8,128)}, f32[3,32,512]{2,1,0:T(8,128)}, u32[]{:S(2)}, u32[]{:S(2)}) collective-permute-start(f32[3,32,512]{2,1,0:T(8,128)} %pad_maximum_fusion.2), channel_id=1, source_target_pairs={{0,1},{1,0},{2,3},{3,2},{4,5},{5,4},{6,7},{7,6},{8,9},{9,8},{10,11... | collective-permute-start | bytes 589832 | tf_op jit(solution)/shard_map/while/body/eval_jaxpr/ppermute | solution.py:104
  196.6 2.1 copy-start.4
  217.8 0.8 copy-start.5
  217.8 1.0 copy-start.2
  217.8 1.1 copy-start.3
  223.0 0.8 copy-start.1
  224.8 7.4 %collective-permute-start.1 = (f32[3,32,512]{2,1,0:T(8,128)S(1)}, f32[3,32,512]{2,1,0:T(8,128)S(1)}, u32[]{:S(2)}, u32[]{:S(2)}) collective-permute-start(f32[3,32,512]{2,1,0:T(8,128)S(1)} %fusion.36), channel_id=1, source_target_pairs={{0,2},{1,3},{2,0},{3,1},{4,6},{5,7},{6,4},{7,5},{8,10},{9,11},{10,... | collective-permute-start | bytes 589832 | tf_op jit(solution)/shard_map/while/body/eval_jaxpr/ppermute | solution.py:104
  233.1 27.9 %collective-permute-start.2 = (f32[3,32,512]{2,1,0:T(8,128)S(1)}, f32[3,32,512]{2,1,0:T(8,128)S(1)}, u32[]{:S(2)}, u32[]{:S(2)}) collective-permute-start(f32[3,32,512]{2,1,0:T(8,128)S(1)} %fusion.37), channel_id=1, source_target_pairs={{0,4},{1,5},{2,6},{3,7},{4,0},{5,1},{6,2},{7,3},{8,12},{9,13},{10,... | collective-permute-start | bytes 589832 | tf_op jit(solution)/shard_map/while/body/eval_jaxpr/ppermute | solution.py:104
  237.2 26.5 %copy-start.6 = (f32[1,512]{1,0:T(1,128)S(1)}, f32[1,512]{1,0:T(1,128)}, u32[]{:S(2)}) copy-start(f32[1,512]{1,0:T(1,128)} %get-tuple-element.662) | copy-start | bytes 6148 | tf_op jit(solution)/shard_map/while
  237.6 33.2 %copy-start.13 = (f32[1,512]{1,0:T(1,128)S(1)}, f32[1,512]{1,0:T(1,128)}, u32[]{:S(2)}) copy-start(f32[1,512]{1,0:T(1,128)} %get-tuple-element.668) | copy-start | bytes 6148 | tf_op jit(solution)/shard_map/while
  237.6 40.2 %copy-start.7 = (f32[1,512]{1,0:T(1,128)S(1)}, f32[1,512]{1,0:T(1,128)}, u32[]{:S(2)}) copy-start(f32[1,512]{1,0:T(1,128)} %get-tuple-element.667) | copy-start | bytes 6148 | tf_op jit(solution)/shard_map/while
  237.6 40.2 %copy-start.8 = (f32[1,512]{1,0:T(1,128)S(1)}, f32[1,512]{1,0:T(1,128)}, u32[]{:S(2)}) copy-start(f32[1,512]{1,0:T(1,128)} %get-tuple-element.666) | copy-start | bytes 6148 | tf_op jit(solution)/shard_map/while
  237.6 40.2 %copy-start.9 = (f32[1,512]{1,0:T(1,128)S(1)}, f32[1,512]{1,0:T(1,128)}, u32[]{:S(2)}) copy-start(f32[1,512]{1,0:T(1,128)} %get-tuple-element.663) | copy-start | bytes 6148 | tf_op jit(solution)/shard_map/while
  237.6 40.2 %copy-start.10 = (f32[1,512]{1,0:T(1,128)S(1)}, f32[1,512]{1,0:T(1,128)}, u32[]{:S(2)}) copy-start(f32[1,512]{1,0:T(1,128)} %get-tuple-element.671) | copy-start | bytes 6148 | tf_op jit(solution)/shard_map/while
  237.6 40.2 %copy-start.11 = (f32[1,512]{1,0:T(1,128)S(1)}, f32[1,512]{1,0:T(1,128)}, u32[]{:S(2)}) copy-start(f32[1,512]{1,0:T(1,128)} %get-tuple-element.670) | copy-start | bytes 6148 | tf_op jit(solution)/shard_map/while
  237.7 40.2 %copy-start.12 = (f32[1,512]{1,0:T(1,128)S(1)}, f32[1,512]{1,0:T(1,128)}, u32[]{:S(2)}) copy-start(f32[1,512]{1,0:T(1,128)} %get-tuple-element.669) | copy-start | bytes 6148 | tf_op jit(solution)/shard_map/while
  261.0 7.1 %collective-permute-start.3 = (f32[3,32,512]{2,1,0:T(8,128)S(1)}, f32[3,32,512]{2,1,0:T(8,128)S(1)}, u32[]{:S(2)}, u32[]{:S(2)}) collective-permute-start(f32[3,32,512]{2,1,0:T(8,128)S(1)} %add.313), channel_id=1, source_target_pairs={{0,8},{1,9},{2,10},{3,11},{4,12},{5,13},{6,14},{7,15},{8,0},{9,1},... | collective-permute-start | bytes 589832 | tf_op jit(solution)/shard_map/while/body/eval_jaxpr/ppermute | solution.py:104
  268.2 9.6 %collective-permute-start.4 = (f32[3,32,512]{2,1,0:T(8,128)S(1)}, f32[3,32,512]{2,1,0:T(8,128)S(1)}, u32[]{:S(2)}, u32[]{:S(2)}) collective-permute-start(f32[3,32,512]{2,1,0:T(8,128)S(1)} %add.314), channel_id=1, source_target_pairs={{0,16},{1,17},{2,18},{3,19},{4,20},{5,21},{6,22},{7,23},{8,24},{9,... | collective-permute-start | bytes 589832 | tf_op jit(solution)/shard_map/while/body/eval_jaxpr/ppermute | solution.py:104
